TPU v7x, 256 devices: a whole 4x4x8 slice. The times are simulated.
256 devices in a mesh: gr: 16 (over z, core), gc: 16 (over x, y).
Axes of the slice: x: 4, y: 4, z: 8, core: 2. Of those that a mesh axis runs over, the one named last changes fastest.
Arguments:
- projectors: bfloat16 [2, 65536, 9216], P(None, ('gr', 'gc')), may hold values from -0.046875 to 0.046875
- wavefunctions: bfloat16 [2, 65536, 512], P(None, ('gr', 'gc')), may hold values from -6 to 6
- coupling: float32 [512, 18, 18], P('gc'), may hold values from -1.5 to 1.5
- atom_order: int32 [512], replicated, may hold values from 0 to 511, each once
Outputs:
- coupled: float32 [9216, 512], P('gc', 'gr')
Inputs may be any that keep to these rules, and one draw needn't show every extreme that they name: `atom_order`: a permutation of the atoms.
All inputs are finite; a program needn't handle non-finite values.
Results may differ from a plain program's by a relative error of at most 0.0003.
Values sent between devices are 32-bit elements; how exact they have to be, the bound alone decides.
A program may use at most 128 MiB of HBM per device.

v0:
```python
import jax
import jax.numpy as jnp
from jax import lax
from jax.sharding import PartitionSpec as P

ATOMS = 512
NH = 18
BANDS = 512
NKB = 9216


def split_up(x, dim, devices):
    before, after = (x.shape[:dim], x.shape[dim + 1 :])
    return jnp.moveaxis(x.reshape(*before, devices, -1, *after), dim, 0)


def summed_on_arrival(x, axis, dim):
    blocks = split_up(x, dim, lax.axis_size(axis))
    arrived = lax.all_to_all(blocks, axis, split_axis=0, concat_axis=0, tiled=True)
    return arrived.sum(axis=0)


def shards(projectors, wavefunctions, coupling, atom_order):
    rows_here = projectors.shape[1]
    shaped = projectors.reshape(2, rows_here, ATOMS, NH)
    waves = wavefunctions.reshape(2 * rows_here, BANDS)
    columns_all = jnp.take(shaped, atom_order, axis=2).reshape(2 * rows_here, NKB)
    term = lax.dot_general(
        waves, columns_all, (((0,), (0,)), ((), ())), preferred_element_type=jnp.float32
    )
    partial_bands = lax.psum_scatter(2.0 * term, "gr", scatter_dimension=0, tiled=True)
    becp = jnp.transpose(summed_on_arrival(partial_bands, "gc", 1))
    local_atoms = coupling.shape[0]
    becp = becp.reshape(local_atoms, NH, becp.shape[1])
    coupled = jnp.einsum("kij,kjb->kib", coupling, becp, precision=lax.Precision.HIGHEST)
    return coupled.reshape(local_atoms * NH, becp.shape[2])


def solution(mesh):
    return jax.shard_map(
        shards,
        mesh=mesh,
        in_specs=(
            P(None, ("gr", "gc"), None),
            P(None, ("gr", "gc"), None),
            P("gc", None, None),
            P(),
        ),
        out_specs=P("gc", "gr"),
        check_vma=False,
    )
```

profile of v0, /device:TPU:1, one launch (start us, length us, event | category | flops | bytes accessed | tf_op | source)
XLA Modules:
  0.0 262.9 jit_solution(8581957452836739234)
XLA Ops:
  6.5 0.0 copy-start
  6.5 0.0 reduce-scatter.4.cloned.1.call-start
  6.5 0.7 compare_select_fusion
  7.3 0.7 compare_and_fusion
  8.0 23.5 %copy.11 = bf16[2,256,9216]{1,0,2:T(2,128)(2,1)} copy(bf16[2,256,9216]{2,1,0:T(8,128)(2,1)} %param.4) | data formatting | bytes 18874368 | tf_op args[0]
  31.4 32.8 %gather_fusion = bf16[512,2,256,18]{2,1,3,0:T(2,128)(2,1)} fusion(bf16[2,256,512,18]{1,0,3,2:T(2,128)(2,1)} %bitcast.21, s32[1024]{0:T(1024)S(1)} %pad_clamp_fusion), kind=kCustom, calls=%fused_computation | custom fusion | bytes 18876416 | tf_op jit(solution)/shard_map/jit(_take)/gather | solution.py:27
  64.2 13.2 %broadcast_select_fusion = bf16[512,2,256,18]{2,1,3,0:T(2,128)(2,1)S(1)} fusion(bf16[512,2,256,18]{2,1,3,0:T(2,128)(2,1)} %gather_fusion, pred[512]{0:T(512)(128)(4,1)S(1)} %compare_and_fusion), kind=kLoop, calls=%fused_computation.2 | loop fusion | flops 4718592 | bytes 18874880 | tf_op jit(solution)/shard_map/jit(_take)/select_n | solution.py:27
  77.5 2.8 %copy.23 = bf16[1152,8,2,256]{3,1,2,0:T(8,128)(2,1)S(1)} copy(bf16[1152,8,2,256]{3,2,1,0:T(2,128)(2,1)S(1)} %bitcast.23) | data formatting | bytes 18874368
  80.2 0.0 copy-done
  80.2 9.1 %multiply_bitcast_fusion = f32[512,9216]{0,1:T(8,128)} fusion(bf16[512,9216]{0,1:T(8,128)(2,1)S(1)} %bitcast.22, bf16[512,512]{1,0:T(8,128)(2,1)S(1)} %bitcast.20), kind=kOutput, calls=%fused_computation.1 | convolution fusion | flops 4836556800 | bytes 28835840 | tf_op jit(solution)/shard_map/dot_general | solution.py:28
  89.3 18.6 %copy.20 = f32[512,9216]{1,0:T(8,128)} copy(f32[512,9216]{0,1:T(8,128)} %multiply_bitcast_fusion) | data formatting | bytes 37748736
  108.0 0.0 reduce-scatter.4.cloned.1.call-update
  108.0 0.0 copy-start.1
  108.0 114.0 %reduce-scatter.4.cloned.1.call-done = f32[32,9216]{1,0:T(8,128)} async-done(((f32[512,9216]{1,0:T(8,128)}), f32[32,9216]{1,0:T(8,128)}) %reduce-scatter.4.cloned.1.call-update) | async-done | bytes 1179664
  222.1 3.9 %copy.21 = f32[32,9216]{0,1:T(8,128)} copy(f32[32,9216]{1,0:T(8,128)} %reduce-scatter.4.cloned.1.call-done) | data formatting | bytes 2359296
  225.9 4.0 %copy.12 = f32[32,16,576]{2,0,1:T(8,128)} copy(f32[32,16,576]{0,2,1:T(8,128)} %bitcast.24) | data formatting | bytes 2359296 | tf_op jit(solution)/shard_map/reshape | solution.py:14
  229.9 6.5 %all-to-all-start = ((f32[16,32,576]{2,1,0:T(8,128)}), f32[16,32,576]{2,1,0:T(8,128)S(1)}, u32[]{:S(2)}, u32[]{:S(2)}) async-start(f32[16,32,576]{2,1,0:T(8,128)} %bitcast.5), calls=%async_computation | async-start | bytes 2621440 | tf_op jit(solution)/shard_map/all_to_all | solution.py:19
  236.4 0.0 copy-done.1
  236.4 0.2 copy.16
  236.7 17.6 %all-to-all-done = f32[16,32,576]{2,1,0:T(8,128)S(1)} async-done(((f32[16,32,576]{2,1,0:T(8,128)}), f32[16,32,576]{2,1,0:T(8,128)S(1)}, u32[]{:S(2)}, u32[]{:S(2)}) %all-to-all-start) | async-done | bytes 1179680 | tf_op jit(solution)/shard_map/all_to_all | solution.py:19
  254.2 0.1 reduce_sum.9
  254.3 0.1 copy.22
  254.5 0.8 convolution_bitcast_fusion
  255.3 0.8 copy.19
  (3 shorter events, 0.1 us)
Async XLA Ops:
  6.5 73.7 %copy-start = (bf16[2,256,512]{2,1,0:T(8,128)(2,1)S(1)}, bf16[2,256,512]{2,1,0:T(8,128)(2,1)}, u32[]{:S(2)}) copy-start(bf16[2,256,512]{2,1,0:T(8,128)(2,1)} %param.5) | copy-start | bytes 1572868
  6.5 215.5 %reduce-scatter.4.cloned.1.call-start = ((), (), s32[]{:S(2)}) async-start(), calls=%async_computation.2 | async-start | bytes 20054016
  108.0 128.4 %copy-start.1 = (f32[32,18,18]{0,2,1:T(8,128)S(1)}, f32[32,18,18]{0,2,1:T(8,128)}, u32[]{:S(2)}) copy-start(f32[32,18,18]{0,2,1:T(8,128)} %param.6) | copy-start | bytes 124420
  229.9 24.3 %all-to-all-start = ((f32[16,32,576]{2,1,0:T(8,128)}), f32[16,32,576]{2,1,0:T(8,128)S(1)}, u32[]{:S(2)}, u32[]{:S(2)}) async-start(f32[16,32,576]{2,1,0:T(8,128)} %bitcast.5), calls=%async_computation | async-start | bytes 2621440 | tf_op jit(solution)/shard_map/all_to_all | solution.py:19
Sparse Core Ops, SparseCore 0:
  108.1 113.8 reduce-scatter.3
where the time goes:
time: 266 us; the launch traced here: 263 us
  waiting for transfers between devices  132 us (50%)
  local copies, waits for them, and re-layouts  86.7 us (33%)
  other arithmetic  14.7 us (6%)
  between operations  13.5 us (5%)
  matrix products  9.84 us (4%)
  starting transfers between devices  6.53 us (2%)
    unnamed x2, waiting for transfers between devices  114 us
    unnamed x10, local copies, waits for them, and re-layouts  49.1 us
    gather x1, local copies, waits for them, and re-layouts, shards(): jnp.take(shaped, atom_order, axis=2).reshape(2 * rows_here, NKB)  32.8 us
    all_to_all x1, waiting for transfers between devices, summed_on_arrival(): lax.all_to_all(blocks, axis, split_axis=0, concat_axis=0, tiled=True)  17.6 us
    select_n x2, other arithmetic, shards(): jnp.take(shaped, atom_order, axis=2).reshape(2 * rows_here, NKB)  14 us
    dot_general x1, matrix products, shards(): lax.dot_general(waves, columns_all, (((0,), (0,)), ((), ())), preferred_e...  9.09 us
    all_to_all x1, starting transfers between devices, summed_on_arrival(): lax.all_to_all(blocks, axis, split_axis=0, concat_axis=0, tiled=True)  6.53 us
  transfers between devices with their start and end apart: 2, of which 2 were waited for; matrix products, arithmetic and copies ran while one was open for 0% of the time, Pallas kernels for 0%

commit v1 on v0

v1 whole, which is shorter than its diff:
```python
import functools

import jax
import jax.numpy as jnp
from jax import lax
from jax.experimental import pallas as pl
from jax.experimental.pallas import tpu as pltpu
from jax.sharding import PartitionSpec as P

ATOMS = 512
NH = 18
BANDS = 512
NKB = 9216
KLOC = 512
MC = 512


def fold4(v):
    lane = lax.broadcasted_iota(jnp.int32, v[0].shape, 1)
    low = lane < 64
    even = (lane // 32) % 2 == 0
    roll = pltpu.roll
    lo = [jnp.where(low, v[q], roll(v[q + 2], 64, 1)) for q in range(2)]
    hi = [jnp.where(low, roll(v[q], 64, 1), v[q + 2]) for q in range(2)]
    u = []
    for a, b in (lo, hi):
        u.append(jnp.where(even, a, roll(b, 32, 1)))
        u.append(jnp.where(even, roll(a, 96, 1), b))
    return u


def local_kernel(order_ref, a_ref, w_ref, out_ref, p_ref, u_ref, a_v, asem, osem):
    cp = pltpu.make_async_copy(a_ref, a_v, asem)
    cp.start()
    cp.wait()
    for h in range(2):
        @pl.loop(0, NKB // MC)
        def _(m):
            lhs = a_v[:, pl.ds(pl.multiple_of(m * MC, MC), MC)]
            r = lax.dot_general(lhs, w_ref[:, h * 256:(h + 1) * 256], (((0,), (0,)), ((), ())),
                                preferred_element_type=jnp.float32)
            rows = pl.ds(pl.multiple_of(m * MC, MC), MC)
            p_ref[0, rows, :] = r[:, :128]
            p_ref[1, rows, :] = r[:, 128:]

        @pl.loop(0, 16)
        def _(gc):
            @pl.loop(0, 2)
            def _(t):
                for s in range(8):
                    v = []
                    for q in range(4):
                        start = order_ref[gc * 32 + q * 8 + s] * NH
                        v.append(p_ref[t, pl.ds(start, 24), :])
                    u = fold4(v)
                    n = 24 if s < 7 else 18
                    for d in range(4):
                        u_ref[h * 8 + t * 4 + d, gc, s * 18:s * 18 + n, :] = u[d][:n]
        pltpu.make_async_copy(u_ref.at[pl.ds(h * 8, 8)], out_ref.at[pl.ds(h * 8, 8)], osem.at[h]).start()
    for h in range(2):
        pltpu.make_async_copy(u_ref.at[pl.ds(h * 8, 8)], out_ref.at[pl.ds(h * 8, 8)], osem.at[h]).wait()


def local_units(order, a, w):
    return pl.pallas_call(
        local_kernel,
        out_shape=jax.ShapeDtypeStruct((16, 16, 144, 128), jnp.float32),
        in_specs=[
            pl.BlockSpec(memory_space=pltpu.SMEM),
            pl.BlockSpec(memory_space=pl.ANY),
            pl.BlockSpec(memory_space=pltpu.VMEM),
        ],
        out_specs=pl.BlockSpec(memory_space=pl.ANY),
        scratch_shapes=[
            pltpu.VMEM((2, NKB + 8, 128), jnp.float32),
            pltpu.VMEM((16, 16, 144, 128), jnp.float32),
            pltpu.VMEM((KLOC, NKB), jnp.bfloat16),
            pltpu.SemaphoreType.DMA,
            pltpu.SemaphoreType.DMA((2,)),
        ],
        compiler_params=pltpu.CompilerParams(vmem_limit_bytes=60 * 2**20),
        cost_estimate=pl.CostEstimate(flops=2 * KLOC * NKB * BANDS, bytes_accessed=30 * 2**20, transcendentals=0),
    )(order, a, w)


def shards(projectors, wavefunctions, coupling, atom_order):
    a = projectors.reshape(KLOC, NKB)
    w = wavefunctions.reshape(KLOC, BANDS)
    units = local_units(atom_order, a, w)
    units = units.reshape(256, 144, 128)
    mine = lax.psum_scatter(units, ("gr", "gc"), scatter_dimension=0, tiled=True)
    mine = 2.0 * mine.reshape(8, NH, 4, 32).transpose(2, 0, 1, 3).reshape(32, NH, 32)
    coupled = jnp.einsum("kij,kjb->kib", coupling, mine, precision=lax.Precision.HIGHEST)
    return coupled.reshape(576, 32)


def solution(mesh):
    return jax.shard_map(
        shards,
        mesh=mesh,
        in_specs=(
            P(None, ("gr", "gc"), None),
            P(None, ("gr", "gc"), None),
            P("gc", None, None),
            P(),
        ),
        out_specs=P("gc", "gr"),
        check_vma=False,
    )
```

time: 266 us -> 520 us (1.95)
  waiting for transfers between devices: 132 us -> 449 us
  local copies, waits for them, and re-layouts: 86.7 us -> 1.25 us
  Pallas kernels: 0 us -> 51.1 us
  other arithmetic: 14.7 us -> 0.89 us
  matrix products: 9.84 us -> 0.76 us
  starting transfers between devices: 6.53 us -> 0.01 us
    reduce_scatter x0 -> x1, waiting for transfers between devices: none -> 449 us  [shards(): lax.psum_scatter(units, ('gr', 'gc'), scatter_dimension=0, tiled=True)]
    unnamed x2 -> x1, waiting for transfers between devices: 114 us -> 0.02 us
    pallas_call x0 -> x1, Pallas kernels: none -> 51.1 us  [local_units(): pl.pallas_call(local_kernel, out_shape=jax.ShapeDtypeStruct((16, 16, 144,...]
    unnamed x10 -> x3, local copies, waits for them, and re-layouts: 49.1 us -> 0.23 us
    gather x1 -> x0, local copies, waits for them, and re-layouts: 32.8 us -> none  [shards(): jnp.take(shaped, atom_order, axis=2).reshape(2 * rows_here, NKB)]
    all_to_all x1 -> x0, waiting for transfers between devices: 17.6 us -> none  [summed_on_arrival(): lax.all_to_all(blocks, axis, split_axis=0, concat_axis=0, tiled=True)]
    select_n x2 -> x0, other arithmetic: 14 us -> none  [shards(): jnp.take(shaped, atom_order, axis=2).reshape(2 * rows_here, NKB)]
    dot_general x2 -> x1, matrix products: 9.84 us -> 0.76 us  [shards(): jnp.einsum('kij,kjb->kib', coupling, mine, precision=lax.Precision.HIGHEST)]
  transfers between devices with their start and end apart: 2 -> 1, of which waited for: 2 -> 1; matrix products, arithmetic and copies ran while one was open for 0% -> 0% of each run, Pallas kernels for 0% -> 0%
where the time goes in v1:
time: 520 us; the launch traced here: 516 us
  waiting for transfers between devices  449 us (86%)
  Pallas kernels  51.1 us (10%)
  between operations  13.4 us (3%)
    reduce_scatter x1, waiting for transfers between devices, shards(): lax.psum_scatter(units, ('gr', 'gc'), scatter_dimension=0, tiled=True)  449 us
    pallas_call x1, Pallas kernels, local_units(): pl.pallas_call(local_kernel, out_shape=jax.ShapeDtypeStruct((16, 16, 144,...  51.1 us
  transfers between devices with their start and end apart: 1, of which 1 were waited for; matrix products, arithmetic and copies ran while one was open for 0% of the time, Pallas kernels for 0%

profile of v1, /device:TPU:1, one launch (start us, length us, event | category | flops | bytes accessed | tf_op | source)
XLA Modules:
  0.0 516.5 jit_solution(5844701988908124205)
XLA Ops:
  6.5 0.0 reduce-scatter.2.cloned.1.call-start
  6.5 0.0 copy-start
  6.5 51.1 %shard_map.46 = f32[16,16,144,128]{3,2,1,0:T(8,128)} custom-call(s32[512]{0:T(512)} %order_ref.1, bf16[512,9216]{1,0:T(8,128)(2,1)} %bitcast.11, bf16[512,512]{1,0:T(8,128)(2,1)} %bitcast.13), custom_call_target="tpu_custom_call" | custom-call | flops 4831838208 | bytes 31457280 | tf_op jit(solution)/shard_map/pallas_call | solution.py:65
  57.6 0.0 reduce-scatter.2.cloned.1.call-update
  57.6 0.0 copy-done
  57.6 0.2 copy.9
  57.9 449.0 %reduce-scatter.2.cloned.1.call-done = f32[1,144,128]{2,1,0:T(8,128)} async-done(((f32[256,144,128]{2,1,0:T(8,128)}), f32[1,144,128]{2,1,0:T(8,128)}) %reduce-scatter.2.cloned.1.call-update) | async-done | bytes 73744 | tf_op jit(solution)/shard_map/reduce_scatter | solution.py:91
  506.9 0.9 broadcast_multiply_fusion
  507.8 0.2 mul.17
  508.0 0.8 convolution_bitcast_fusion
  508.8 0.8 copy.11
  (2 shorter events, 0.1 us)
Async XLA Ops:
  6.5 500.4 %reduce-scatter.2.cloned.1.call-start = ((), (), s32[]{:S(2)}) async-start(), calls=%async_computation.1 | async-start | bytes 18948096 | tf_op jit(solution)/shard_map/reduce_scatter | solution.py:91
  6.5 51.1 %copy-start = (f32[32,18,18]{0,2,1:T(8,128)S(1)}, f32[32,18,18]{0,2,1:T(8,128)}, u32[]{:S(2)}) copy-start(f32[32,18,18]{0,2,1:T(8,128)} %param.6) | copy-start | bytes 124420
Sparse Core Ops, SparseCore 0:
  57.8 449.1 reduce-scatter.1

commit v2 on v0

v2 whole, which is shorter than its diff:
```python
import jax
import jax.numpy as jnp
from jax import lax
from jax.experimental import pallas as pl
from jax.experimental.pallas import tpu as pltpu
from jax.sharding import PartitionSpec as P

MESH = pl.DeviceIdType.MESH
NH = 18
BANDS = 512
NKB = 9216
KLOC = 512
MC = 1152
CHUNKS = NKB // MC
ROWS = ((0, 48), (48, 96), (96, 144))
SCHEDULE = (
    "m0", "bar", "g0", "ds0", "g1", "ds1", "m1.0", "dw02", "c1.0.L0", "c1.1.L0", "m1.1", "dw00", "c1.2.L0", "c1.3.L0",
    "a1.0.L", "a1.0.S", "a1.1.L", "a1.1.S", "m1.2", "dw01", "b1.0.L", "b1.0.S", "b1.1.L", "b1.1.S", "m1.3", "dw12",
    "c1.0.f1", "c1.0.S0", "c1.1.S0", "g2", "ds2", "c1.1.f1", "dw10", "c1.2.S0", "a1.2.L", "a1.2.S", "a1.3.L",
    "a1.3.S", "g3", "ds3", "c1.2.f1", "dw11", "a1.0.1", "b1.2.L", "b1.2.S", "b1.3.L", "b1.3.S", "cb0", "c1.3.S0",
    "cb1", "c1.3.f1", "dw22", "b1.0.1", "cb2", "a1.1.1", "cb3", "c1.0.n1", "dw20", "a1.4.S", "a1.5.S", "cb4", "cb5",
    "c1.0.f2", "dw21", "b1.1.1", "b1.4.S", "b1.5.S", "a1.2.1", "dw32", "c1.1.n1", "c1.1.f2", "b1.2.1", "dw30",
    "a1.6.S", "a1.3.1", "a1.7.S", "dw31", "b1.6.S", "c1.2.n1", "b1.3.1", "c1.2.f2", "b1.7.S", "a1.0.E", "a1.4.L",
    "c1.3.n1", "b1.0.E", "c1.3.f2", "b1.4.L", "a1.1.E", "a2.0.L", "a2.0.S", "a1.5.L", "c1.0.n2", "c1.0.f3", "b1.1.E",
    "b2.0.L", "b2.0.S", "a1.2.E", "b1.5.L", "c1.1.n2", "a1.6.L", "c1.1.f3", "b1.2.E", "a1.3.E", "a2.1.L", "a2.1.S",
    "a1.7.L", "c1.2.n2", "b1.3.E", "b2.1.L", "b2.1.S", "c1.2.f3", "b1.6.L", "a1.4.1", "b1.7.L", "c1.3.n2", "a1.5.1",
    "b2.0.1", "b1.4.1", "c1.3.f3", "a2.0.1", "a1.6.1", "b1.5.1", "a2.1.1", "c1.0.E", "c2.0.L", "c2.1.L", "a1.7.1",
    "b2.1.1", "b1.6.1", "a1.4.E", "c1.1.E", "c2.0.S", "c2.1.S", "b1.7.1", "a1.5.E", "a2.2.L", "a2.2.S", "b1.4.E",
    "b2.0.E", "b3.0.L0", "a2.0.E", "a3.0.L0", "c1.2.E", "a1.6.E", "b1.5.E", "b2.2.L", "b2.2.S", "a2.1.E", "a3.0.S0",
    "c2.0.1", "c1.3.E", "a3.0.f1", "c2.1.1", "b1.6.E", "b1.7.E", "b2.3.L", "b2.3.S", "a1.7.E", "a2.3.L", "a2.3.S",
    "a2.2.1", "b2.1.E", "b3.0.S0", "b3.0.f1", "b2.2.1", "c2.0.E", "c3.0.L", "c3.0.S", "c2.1.E", "b2.3.1", "a2.3.1",
    "b2.2.E", "b3.0.f2", "b3.0.n1", "a2.2.E", "a3.0.f2", "a3.0.n1", "c3.0.1", "b2.3.E", "a2.3.E", "b3.0.f3",
    "b3.0.n2", "c3.0.E", "a3.0.f3", "a3.0.n2", "b3.0.E", "a3.0.E",
)


def fold4(v):
    lane = lax.broadcasted_iota(jnp.int32, v[0].shape, 1)
    low = lane < 64
    even = (lane // 32) % 2 == 0
    roll = pltpu.roll
    lo = [jnp.where(low, v[q], roll(v[q + 2], 64, 1)) for q in range(2)]
    hi = [jnp.where(low, roll(v[q], 64, 1), v[q + 2]) for q in range(2)]
    u = []
    for a, b in (lo, hi):
        u.append(jnp.where(even, a, roll(b, 32, 1)))
        u.append(jnp.where(even, roll(a, 96, 1), b))
    return u


def kernel(order_hbm, a_hbm, w_hbm, c_hbm, o_ref,
           p_ref, u_ref, d_ref, a_v, w_v, c_v, g_ref, pk, rk, t_ref,
           ra1, rb1, rc1, ra2, rb2, rc2, ra3, rb3, rc3,
           order, asem, wsem, csem, osem, ds_s, ds_r,
           a1s, a1r, b1s, b1r, c1s, c1r, a2s, a2r, b2s, b2r, c2s, c2r,
           a3s, a3r, b3s, b3r, c3s, c3r, ks_s, ks_r):
    gr, gc = lax.axis_index("gr"), lax.axis_index("gc")
    z, core = gr // 2, gr % 2
    x, y = gc // 4, gc % 4
    sg = 1 - 2 * core
    par = z % 2
    zt = z // 2
    quarter = par * 2 + core

    def xdev(d):
        return (gr, ((x + d + 4) % 4) * 4 + y)

    def ydev(d):
        return (gr, x * 4 + (y + d + 4) % 4)

    def zdev(d):
        return (((z + d + 8) % 8) * 2 + core, gc)

    partner = (gr + sg, gc)
    zpair = z + 1 - 2 * par
    pairdev = (zpair * 2 + core, gc)
    diagdev = (zpair * 2 + 1 - core, gc)

    tiles = [(zt + 2) % 4, (zt + 1 + 2 * par) % 4, (zt + 3 - 2 * par) % 4, zt]

    def kof(d):
        rel = ((par + d + 8) // 2) % 4
        odd = rel % 2
        half = rel // 2
        pos = odd * (1 + (par + half) % 2) + (1 - odd) * (3 - 3 * half)
        return 2 * pos + (par + d + 8) % 2

    kme = 6 + par

    def acopy(m):
        cols = pl.ds(pl.multiple_of(m * MC, 128), MC)
        return pltpu.make_async_copy(a_hbm.at[:, cols], a_v.at[:, cols], asem.at[m])

    def wcopy(t):
        return pltpu.make_async_copy(w_hbm.at[:, pl.ds(t * 128, 128)], w_v.at[t], wsem.at[t])

    with jax.named_scope("start"):
        for t in range(4):
            wcopy(t).start()
        acopy(0).start()
        ocopy = pltpu.make_async_copy(order_hbm, order, osem)
        ccopy = pltpu.make_async_copy(c_hbm, c_v, csem)
        barrier = pltpu.get_barrier_semaphore()
        greet = [xdev(1), xdev(-1), ydev(1), ydev(-1), zdev(1), zdev(-1), partner, diagdev]
        for dev in greet:
            pl.semaphore_signal(barrier, inc=1, device_id=dev, device_id_type=MESH)
    with jax.named_scope("waitw"):
        for t in range(4):
            wcopy(t).wait()
        acopy(1).start()
        acopy(2).start()
        ocopy.start()

    def matmul(h, first, last, wait):
        w = jnp.concatenate([w_v[tiles[2 * h]], w_v[tiles[2 * h + 1]]], axis=1)

        @pl.loop(first, last)
        def _(m):
            if wait:
                acopy(m).wait()

                @pl.when(m + 3 < CHUNKS)
                def _():
                    acopy(m + 3).start()
            lhs = a_v[:, pl.ds(pl.multiple_of(m * MC, 128), MC)]
            r = lax.dot_general(lhs, w, (((0,), (0,)), ((), ())), preferred_element_type=jnp.float32)
            rows = pl.ds(pl.multiple_of(m * MC, 128), MC)
            p_ref[0, rows, :] = r[:, :128]
            p_ref[1, rows, :] = r[:, 128:]

    def gather(kk):
        @pl.loop(0, 16)
        def _(g):
            for q in range(4):
                way = 1 - 2 * (q % 2)
                rx = (way * (g // 4 - x) + 4) % 4
                ry = (way * (g % 4 - y) + 4) % 4
                for s in range(8):
                    start = order[g * 32 + q * 8 + s] * NH
                    n = 24 if s < 7 else 18
                    u_ref[2 * kk + q // 2, q % 2, rx, ry, s * 18:s * 18 + n, :] = (
                        p_ref[kk % 2, pl.ds(start, n), :])

    def remote(src, dst, ssem, rsem, dev):
        return pltpu.make_async_remote_copy(src_ref=src, dst_ref=dst, send_sem=ssem, recv_sem=rsem,
                                            device_id=dev, device_id_type=MESH)

    def dcopy(kk, c):
        r0, r1 = ROWS[c]
        ks = pl.ds(2 * kk, 2)
        return remote(u_ref.at[ks, 1 - core, :, :, r0:r1, :], d_ref.at[ks, :, :, r0:r1, :],
                      ds_s, ds_r.at[kk, c], partner)

    def dsend(kk):
        for c in (2, 0, 1):
            dcopy(kk, c).start()

    def ring4(own, add, slot, ssem, rsem, dev):
        def copy(j):
            return remote(own((2, 1, 3)[j]), slot(j), ssem, rsem(min(j, 1)), dev(-sg if j == 2 else sg))

        def far():
            add(2, [])
            copy(0).start()

        def back():
            add(3, [])
            copy(2).start()

        def second():
            copy(0).wait_recv()
            add(1, [slot(0)])
            copy(1).start()

        def end():
            remote(slot(pl.ds(1, 2)), slot(pl.ds(1, 2)), ssem, rsem(1), dev(sg)).wait_recv()
            add(0, [slot(1), slot(2)])

        return {"L": far, "S": back, "1": second, "E": end}

    def ring8(own, add, slot, ssem, rsem):
        far = {0: 4 * sg, 1: 3 * sg, 2: 2 * sg, 3: sg, 5: -3 * sg, 6: -2 * sg, 4: -sg}
        sem = {0: 0, 1: 1, 2: 2, 3: 3, 4: 3, 5: 4, 6: 5}

        def copy(j):
            return remote(own(far[j]), slot(j), ssem, rsem(sem[j]), zdev(sg if j < 4 else -sg))

        def start(j):
            def run():
                add(far[j], [])
                copy(j).start()
            return run

        def step(before, j):
            def run():
                copy(before).wait_recv()
                add(far[j], [slot(before)])
                copy(j).start()
            return run

        def end():
            remote(slot(pl.ds(3, 2)), slot(pl.ds(3, 2)), ssem, rsem(3), zdev(sg)).wait_recv()
            add(0 * sg, [slot(3), slot(4)])

        return {"L0": start(0), "S0": start(5), "f1": step(0, 1), "f2": step(1, 2), "f3": step(2, 3),
                "n1": step(5, 6), "n2": step(6, 4), "E": end}

    def adder(own, more=None):
        def add(dest, extra):
            refs = ([more(dest)] if more is not None else []) + extra
            if refs:
                ref = own(dest)
                total = ref[...]
                for other in refs:
                    total = total + other[...]
                ref[...] = total
        return add

    def rows(c):
        return slice(*ROWS[c])

    def a1(k):
        own = lambda r: u_ref.at[k, core, r, :, rows(0), :]
        more = lambda r: d_ref.at[k, r, :, rows(0), :]
        return ring4(own, adder(own, more), lambda j: ra1.at[j, k],
                     a1s, lambda j: a1r.at[j, k], xdev)

    def b1(k):
        own = lambda r: u_ref.at[k, core, :, r, rows(1), :]
        more = lambda r: d_ref.at[k, :, r, rows(1), :]
        return ring4(own, adder(own, more), lambda j: rb1.at[j, k],
                     b1s, lambda j: b1r.at[j, k], ydev)

    def c1(i):
        r = (2, 3, 1, 0)[i]
        own = lambda d: u_ref.at[kof(d), core, r, :, rows(2), :]
        more = lambda d: d_ref.at[kof(d), r, :, rows(2), :]
        return ring8(own, adder(own, more), lambda j: rc1.at[j, r],
                     c1s, lambda j: c1r.at[j, r])

    def a2(i):
        ks = pl.ds(2 * i, 2)
        own = lambda r: u_ref.at[ks, core, 0, r, rows(0), :]
        return ring4(own, adder(own), lambda j: ra2.at[j, ks],
                     a2s, lambda j: a2r.at[j, i], ydev)

    def b2(i):
        ks = pl.ds(2 * i, 2)
        own = lambda r: u_ref.at[ks, core, r, 0, rows(1), :]
        return ring4(own, adder(own), lambda j: rb2.at[j, ks],
                     b2s, lambda j: b2r.at[j, i], xdev)

    def c2(i):
        ys = pl.ds(2 - 2 * i, 2)
        own = lambda r: u_ref.at[kme, core, r, ys, rows(2), :]
        return ring4(own, adder(own), lambda j: rc2.at[j, ys],
                     c2s, lambda j: c2r.at[j, i], xdev)

    def c3():
        own = lambda r: u_ref.at[kme, core, 0, r, rows(2), :]
        return ring4(own, adder(own), lambda j: rc3.at[j],
                     c3s, lambda j: c3r.at[j], ydev)

    def a3():
        own = lambda d: u_ref.at[kof(d), core, 0, 0, rows(0), :]
        return ring8(own, adder(own), lambda j: ra3.at[j], a3s, lambda j: a3r.at[j])

    def b3():
        own = lambda d: u_ref.at[kof(d), core, 0, 0, rows(1), :]
        return ring8(own, adder(own), lambda j: rb3.at[j], b3s, lambda j: b3r.at[j])

    def spread(i):
        if i == 0:
            ccopy.wait()
        for j in range(3 * i, 3 * i + 3):
            v = 2.0 * c_v[:, j, :]
            v = pltpu.roll(jnp.concatenate([v, v, v, v], axis=1), 128 - 8 * quarter, 1)
            for s in range(8):
                r = (s * NH + j) * 24
                p_ref[0, r:r + NH, :] = jnp.broadcast_to(v[:, s:s + 1], (NH, 128))

    todo = {}
    for k in range(4):
        todo[f"g{k}"] = lambda k=k: gather(k)
        todo[f"ds{k}"] = lambda k=k: dsend(k)
        for c in range(3):
            todo[f"dw{k}{c}"] = lambda k=k, c=c: dcopy(k, c).wait_recv()
        todo[f"m1.{k}"] = lambda k=k: matmul(1, 2 * k, 2 * k + 2, False)
    for name, rings in (("a1", [a1(k) for k in range(8)]), ("b1", [b1(k) for k in range(8)]), ("c1", [c1(i) for i in range(4)]),
                        ("a2", [a2(i) for i in range(4)]), ("b2", [b2(i) for i in range(4)]), ("c2", [c2(i) for i in range(2)]),
                        ("a3", [a3()]), ("b3", [b3()]), ("c3", [c3()])):
        for i, ring in enumerate(rings):
            for step, run in ring.items():
                todo[f"{name}.{i}.{step}"] = run
    todo["m0"] = lambda: matmul(0, 0, CHUNKS, True)
    def bar():
        ocopy.wait()
        ccopy.start()
        pl.semaphore_wait(barrier, len(greet))

    todo["bar"] = bar
    for i in range(6):
        todo[f"cb{i}"] = lambda i=i: spread(i)
    for name in SCHEDULE:
        with jax.named_scope(name):
            todo.pop(name)()
    assert not todo, list(todo)

    with jax.named_scope("couple"):
        for s in range(8):
            acc = None
            for j in range(NH):
                r = s * NH + j
                term = p_ref[0, r * 24:r * 24 + NH, :] * u_ref[kme, core, 0, 0, r:r + 1, :]
                acc = term if acc is None else acc + term
            g_ref[s * NH:s * NH + NH, :] = acc
    with jax.named_scope("pack"):
        for i in range(5):
            v = [g_ref[8 * t:8 * t + 8, :] for t in ((4 * i, 4 * i + 1, 4 * i + 2, 4 * i + 3) if i < 4 else (16, 17, 16, 17))]
            for d, u in enumerate(fold4(v)):
                pk[d, 8 * i:8 * i + 8, :] = u

    def kcopy(rel):
        dev = (partner, pairdev, diagdev)[rel]
        d = (par * 2 + 1 - core, (1 - par) * 2 + core, 3 - quarter)[rel]
        return remote(pk.at[d], rk.at[rel], ks_s, ks_r.at[rel], dev)

    for rel in (2, 1, 0):
        kcopy(rel).start()

    def unpack(ref, q):
        for t in range(18):
            tile = ref[8 * (t // 4):8 * (t // 4) + 8, :]
            if t % 4:
                tile = pltpu.roll(tile, 128 - 32 * (t % 4), 1)
            t_ref[pl.ds(pl.multiple_of(q * 144 + t * 8, 8), 8), :] = tile

    with jax.named_scope("unpack0"):
        unpack(pk.at[quarter], quarter)
    for rel, q in ((0, par * 2 + 1 - core), (1, (1 - par) * 2 + core), (2, 3 - quarter)):
        with jax.named_scope(f"k{rel}"):
            kcopy(rel).wait_recv()
        unpack(rk.at[rel], q)
    with jax.named_scope("turn"):
        o_ref[...] = jnp.transpose(t_ref[...])[:32, :]
    with jax.named_scope("drain"):
        for whole, sem in ((d_ref, ds_s), (ra1, a1s), (rb1, b1s), (rc1, c1s), (ra2, a2s), (rb2, b2s), (rc2, c2s),
                           (ra3, a3s), (rb3, b3s), (rc3, c3s), (rk, ks_s)):
            remote(whole, whole, sem, ks_r.at[0], partner).wait_send()


def shards(projectors, wavefunctions, coupling, atom_order):
    a = projectors.reshape(KLOC, NKB)
    w = wavefunctions.reshape(KLOC, BANDS)
    f32 = jnp.float32
    dma = pltpu.SemaphoreType.DMA
    any_spec = pl.BlockSpec(memory_space=pltpu.HBM)
    sems = []
    for shape in ((2, 8), (2, 8), (6, 4), (2, 4), (2, 4), (2, 2), (6,), (6,), (2,), (3,)):
        sems += [dma, dma(shape)]
    out = pl.pallas_call(
        kernel,
        out_shape=pltpu.VMEM((32, 576), f32),
        in_specs=[any_spec, any_spec, any_spec, any_spec],
        out_specs=pl.BlockSpec(memory_space=pltpu.VMEM),
        scratch_shapes=[
            pltpu.VMEM((2, NKB + 8, 128), f32),
            pltpu.VMEM((8, 2, 4, 4, 144, 128), f32),
            pltpu.VMEM((8, 4, 4, 144, 128), f32),
            pltpu.VMEM((KLOC, NKB), jnp.bfloat16),
            pltpu.VMEM((4, KLOC, 128), jnp.bfloat16),
            pltpu.VMEM((NH, NH, 32), f32),
            pltpu.VMEM((144, 128), f32),
            pltpu.VMEM((4, 40, 128), f32),
            pltpu.VMEM((3, 40, 128), f32),
            pltpu.VMEM((576, 128), f32),
            pltpu.VMEM((3, 8, 4, 48, 128), f32),
            pltpu.VMEM((3, 8, 4, 48, 128), f32),
            pltpu.VMEM((7, 4, 4, 48, 128), f32),
            pltpu.VMEM((3, 8, 48, 128), f32),
            pltpu.VMEM((3, 8, 48, 128), f32),
            pltpu.VMEM((3, 4, 48, 128), f32),
            pltpu.VMEM((7, 48, 128), f32),
            pltpu.VMEM((7, 48, 128), f32),
            pltpu.VMEM((3, 48, 128), f32),
            pltpu.SMEM((512,), jnp.int32),
            dma((CHUNKS,)),
            dma((4,)),
            dma,
            dma,
            dma,
            dma((4, 3)),
        ] + sems,
        compiler_params=pltpu.CompilerParams(
            vmem_limit_bytes=62500000, collective_id=0, has_side_effects=True),
        cost_estimate=pl.CostEstimate(flops=2 * KLOC * NKB * BANDS, bytes_accessed=10 * 2**20, transcendentals=0),
    )(atom_order, a, w, coupling.transpose(1, 2, 0))
    return out.T


def solution(mesh):
    return jax.shard_map(
        shards,
        mesh=mesh,
        in_specs=(
            P(None, ("gr", "gc"), None),
            P(None, ("gr", "gc"), None),
            P("gc", None, None),
            P(),
        ),
        out_specs=P("gc", "gr"),
        check_vma=False,
    )
```

time: 266 us -> 67.2 us (0.25); the launches traced: 263 us -> 67.1 us
  waiting for transfers between devices: 132 us -> 0 us
  local copies, waits for them, and re-layouts: 86.7 us -> 0.64 us
  Pallas kernels: 0 us -> 66.4 us
  other arithmetic: 14.7 us -> 0 us
  between operations: 13.5 us -> 0.01 us
  matrix products: 9.84 us -> 0 us
  starting transfers between devices: 6.53 us -> 0 us
    unnamed x2 -> x0, waiting for transfers between devices: 114 us -> none
    pallas_call x0 -> x1, Pallas kernels: none -> 66.4 us  [shards(): pl.pallas_call(kernel, out_shape=pltpu.VMEM((32, 576), f32), in_specs=[an...]
    unnamed x10 -> x1, local copies, waits for them, and re-layouts: 49.1 us -> 0.64 us
    gather x1 -> x0, local copies, waits for them, and re-layouts: 32.8 us -> none  [shards(): jnp.take(shaped, atom_order, axis=2).reshape(2 * rows_here, NKB)]
    all_to_all x1 -> x0, waiting for transfers between devices: 17.6 us -> none  [summed_on_arrival(): lax.all_to_all(blocks, axis, split_axis=0, concat_axis=0, tiled=True)]
    select_n x2 -> x0, other arithmetic: 14 us -> none  [shards(): jnp.take(shaped, atom_order, axis=2).reshape(2 * rows_here, NKB)]
    dot_general x2 -> x0, matrix products: 9.84 us -> none  [the longest x1 9.09 us: shards(): lax.dot_general(waves, columns_all, (((0,), (0,)), ((), ())), preferred_e...]
    all_to_all x1 -> x0, starting transfers between devices: 6.53 us -> none  [summed_on_arrival(): lax.all_to_all(blocks, axis, split_axis=0, concat_axis=0, tiled=True)]
  transfers between devices with their start and end apart: 2 -> 0, of which waited for: 2 -> 0; matrix products, arithmetic and copies ran while one was open for 0% -> 0% of each run, Pallas kernels for 0% -> 0%
where the time goes in v2:
time: 67.2 us; the launch traced here: 67.1 us
  Pallas kernels  66.4 us (99%)
    pallas_call x1, Pallas kernels, shards(): pl.pallas_call(kernel, out_shape=pltpu.VMEM((32, 576), f32), in_specs=[an...  66.4 us

profile of v2, /device:TPU:1, one launch (start us, length us, event | category | flops | bytes accessed | tf_op | source)
XLA Modules:
  0.0 67.1 jit_solution(2779597753304902763)
XLA Ops:
  0.0 66.4 %shard_map.46 = f32[32,576]{1,0:T(8,128)S(1)} custom-call(s32[512]{0:T(512)} %order_hbm.1, bf16[512,9216]{1,0:T(8,128)(2,1)} %bitcast.5, bf16[512,512]{1,0:T(8,128)(2,1)} %bitcast.6, f32[18,18,32]{2,1,0:T(8,128)} %bitcast.7), custom_call_target="tpu_custom_call" | custom-call | flops 4831838208 | bytes 10485760 | tf_op jit(solution)/shard_map/pallas_call | solution.py:361
  66.4 0.6 copy.6

commit v3 on v2

v3 whole, which is shorter than its diff:
```python
import functools

import jax
import jax.numpy as jnp
from jax import lax
from jax.experimental import pallas as pl
from jax.experimental.pallas import tpu as pltpu
from jax.sharding import PartitionSpec as P

MESH = pl.DeviceIdType.MESH
NH = 18
BANDS = 512
NKB = 9216
KLOC = 512
MC = 1152
CHUNKS = NKB // MC
ROWS = (slice(0, 48), slice(48, 96), slice(96, 144))


def fold4(v):
    lane = lax.broadcasted_iota(jnp.int32, v[0].shape, 1)
    low = lane < 64
    even = (lane // 32) % 2 == 0
    roll = pltpu.roll
    lo = [jnp.where(low, v[q], roll(v[q + 2], 64, 1)) for q in range(2)]
    hi = [jnp.where(low, roll(v[q], 64, 1), v[q + 2]) for q in range(2)]
    u = []
    for a, b in (lo, hi):
        u.append(jnp.where(even, a, roll(b, 32, 1)))
        u.append(jnp.where(even, roll(a, 96, 1), b))
    return u


def kernel(order_hbm, a_hbm, w_hbm, c_hbm, o_ref,
           p_ref, u_ref, d_ref, a_v, w_v, c_v, g_ref, pk, rk, t_ref,
           ra1, rb1, rc1, ra2, rb2, rc2, ra3, rb3, rc3,
           order, asem, wsem, csem, osem, ds_s, ds_r,
           a1s, a1r, b1s, b1r, c1s, c1r, a2s, a2r, b2s, b2r, c2s, c2r,
           a3s, a3r, b3s, b3r, c3s, c3r, ks_s, ks_r):
    gr, gc = lax.axis_index("gr"), lax.axis_index("gc")
    z, core = gr // 2, gr % 2
    x, y = gc // 4, gc % 4
    half = (core + x + y + z) % 2
    sg = 1 - 2 * half
    par = z % 2
    zt = z // 2
    quarter = par * 2 + half

    def xdev(d):
        return (z * 2 + (core + d + 4) % 2, ((x + d + 4) % 4) * 4 + y)

    def ydev(d):
        return (z * 2 + (core + d + 4) % 2, x * 4 + (y + d + 4) % 4)

    def pdev(d):
        return (z * 2 + (core + d + 4) % 2, (1 - half) * xdev(d)[1] + half * ydev(d)[1])

    def qdev(d):
        return (z * 2 + (core + d + 4) % 2, half * xdev(d)[1] + (1 - half) * ydev(d)[1])

    def zdev(d):
        return (((z + d + 8) % 8) * 2 + (core + d + 8) % 2, gc)

    partner = (z * 2 + 1 - core, gc)
    zpair = z + 1 - 2 * par
    pairdev = (zpair * 2 + 1 - core, gc)
    diagdev = (zpair * 2 + core, gc)

    tiles = [(zt + 2) % 4, (zt + 1 + 2 * par) % 4, (zt + 3 - 2 * par) % 4, zt]

    def kof(d):
        rel = ((par + d + 8) // 2) % 4
        odd = rel % 2
        up = rel // 2
        pos = odd * (1 + (par + up) % 2) + (1 - odd) * (3 - 3 * up)
        return 2 * pos + (par + d + 8) % 2

    kme = 6 + par

    def acopy(m):
        cols = pl.ds(pl.multiple_of(m * MC, 128), MC)
        return pltpu.make_async_copy(a_hbm.at[:, cols], a_v.at[:, cols], asem.at[m % 5])

    def wcopy(t):
        cols = pl.ds(pl.multiple_of(tiles[t] * 128, 128), 128)
        return pltpu.make_async_copy(w_hbm.at[:, cols], w_v.at[t], wsem.at[t])

    for t in range(2):
        wcopy(t).start()
    acopy(0).start()
    ocopy = pltpu.make_async_copy(order_hbm, order, osem)
    ccopy = pltpu.make_async_copy(c_hbm, c_v, csem)
    barrier = pltpu.get_barrier_semaphore()
    greet = [xdev(1), xdev(-1), xdev(2), ydev(1), ydev(-1), ydev(2), zdev(1), zdev(-1), zdev(2), zdev(-2), partner, diagdev]
    for dev in greet:
        pl.semaphore_signal(barrier, inc=1, device_id=dev, device_id_type=MESH)
    acopy(1).start()
    for t in range(2):
        wcopy(t).wait()
    for m in range(2, 4):
        acopy(m).start()
    for t in range(2, 4):
        wcopy(t).start()
    ocopy.start()

    def matmul(h, first, last, wait):
        w = jnp.concatenate([w_v[2 * h], w_v[2 * h + 1]], axis=1)

        @pl.loop(first, last)
        def _(m):
            if wait:
                acopy(m).wait()

                @pl.when(m + 4 < CHUNKS)
                def _():
                    acopy(m + 4).start()
            lhs = a_v[:, pl.ds(pl.multiple_of(m * MC, 128), MC)]
            r = lax.dot_general(lhs, w, (((0,), (0,)), ((), ())), preferred_element_type=jnp.float32)
            rows = pl.ds(pl.multiple_of(m * MC, 128), MC)
            p_ref[0, rows, :] = r[:, :128]
            p_ref[1, rows, :] = r[:, 128:]

    def gather(kk, zs):
        @pl.loop(0, 16)
        def _(g):
            for zl in zs:
                for h in range(2):
                    way = 1 - 2 * h
                    rx = (way * (g // 4 - x) + 4) % 4
                    ry = (way * (g % 4 - y) + 4) % 4
                    p, q = (rx, ry) if h == 0 else (ry, rx)
                    for s in range(8):
                        start = order[g * 32 + (2 * zl + h) * 8 + s] * NH
                        n = 24 if s < 7 else 18
                        u_ref[2 * kk + zl, h, p, q, s * 18:s * 18 + n, :] = p_ref[kk % 2, pl.ds(start, n), :]

    def remote(src, dst, ssem, rsem, dev):
        return pltpu.make_async_remote_copy(src_ref=src, dst_ref=dst, send_sem=ssem, recv_sem=rsem,
                                            device_id=dev, device_id_type=MESH)

    def dcopy(kk, c):
        ks = pl.ds(2 * kk, 2)
        return remote(u_ref.at[ks, 1 - half, :, :, ROWS[c], :], d_ref.at[ks, :, :, ROWS[c], :],
                      ds_s, ds_r.at[kk, c], partner)

    def dfirst(h, c):
        k = (par + h) % 2
        return remote(u_ref.at[k, 1 - half, :, :, ROWS[c], :], d_ref.at[k, :, :, ROWS[c], :],
                      ds_s, ds_r.at[4 * h, c], partner)

    def make(kk):
        gather(kk, (0, 1))
        for c in (0, 2, 1):
            dcopy(kk, c).start()

    def make_first(h):
        gather(0, ((par + h) % 2,))
        for c in (0, 2, 1):
            dfirst(h, c).start()

    def ring4(own, add, slot, ssem, rsem, dev, direct=False):
        def copy(j):
            if direct:
                return remote(own((2, 1, 3)[j]), slot(j), ssem, rsem(0), dev((2, sg, -sg)[j]))
            return remote(own((2, 1, 3)[j]), slot(j), ssem, rsem(min(j, 1)), dev(-sg if j == 2 else sg))

        def far():
            add(2, [])
            copy(0).start()

        def back():
            add(3, [])
            copy(2).start()

        def second():
            if not direct:
                copy(0).wait_recv()
                add(1, [slot(0)])
            copy(1).start()

        def end():
            first = 0 if direct else 1
            landed = slot(pl.ds(first, 3 - first))
            remote(landed, landed, ssem, rsem(first), dev(sg)).wait_recv()
            add(0, [slot(j) for j in range(first, 3)])

        return far, back, second, end

    def ring8(own, add, slot, ssem, rsem):
        far = {0: 4 * sg, 1: 3 * sg, 2: 2 * sg, 3: sg, 5: -3 * sg, 6: -2 * sg, 4: -sg}
        sem = {0: 0, 1: 1, 2: 2, 3: 3, 4: 3, 5: 4, 6: 5}

        def copy(j):
            return remote(own(far[j]), slot(j), ssem, rsem(sem[j]), zdev(sg if j < 4 else -sg))

        def start(j):
            def run():
                add(far[j], [])
                copy(j).start()
            return run

        def step(before, j):
            def run():
                copy(before).wait_recv()
                add(far[j], [slot(before)])
                copy(j).start()
            return run

        def end():
            remote(slot(pl.ds(3, 2)), slot(pl.ds(3, 2)), ssem, rsem(3), zdev(sg)).wait_recv()
            add(0 * sg, [slot(3), slot(4)])

        return start(0), start(5), step(0, 1), step(1, 2), step(2, 3), step(5, 6), step(6, 4), end

    def ring8_short(own, add, slot, ssem, rsem):
        far = (4 * sg, 3 * sg, -3 * sg, -2 * sg, 2 * sg, sg, -sg)
        dev = (2 * sg, sg, -2 * sg, -sg, 2 * sg, sg, -sg)
        group = (0, 0, 1, 1, 2, 2, 2)

        def copy(j):
            return remote(own(far[j]), slot(j), ssem, rsem(group[j]), zdev(dev[j]))

        def wait(first, n):
            landed = slot(pl.ds(first, n))
            remote(landed, landed, ssem, rsem(group[first]), zdev(sg)).wait_recv()
            return [slot(j) for j in range(first, first + n)]

        def join(first, j):
            def run():
                add(far[j], wait(first, 2))
                copy(j).start()
            return run

        def end():
            add(0 * sg, wait(4, 3))

        return (copy(0).start, copy(1).start, copy(2).start, copy(3).start, join(0, 4), copy(5).start, join(2, 6), end)

    def adder(own, more=None):
        def add(dest, extra):
            refs = ([more(dest)] if more is not None else []) + extra
            if refs:
                ref = own(dest)
                total = ref[...]
                for other in refs:
                    total = total + other[...]
                ref[...] = total
        return add

    def a1(k):
        at = (par + k) % 2 if k < 2 else k
        own = lambda r: u_ref.at[at, half, r, :, ROWS[0], :]
        more = lambda r: d_ref.at[at, r, :, ROWS[0], :]
        return ring4(own, adder(own, more), lambda j: ra1.at[j, k],
                     a1s, lambda j: a1r.at[j, k], pdev)

    def b1(k):
        at = (par + k) % 2 if k < 2 else k
        own = lambda r: u_ref.at[at, half, :, r, ROWS[1], :]
        more = lambda r: d_ref.at[at, :, r, ROWS[1], :]
        return ring4(own, adder(own, more), lambda j: rb1.at[j, k],
                     b1s, lambda j: b1r.at[j, k], qdev)

    def c1(i):
        r = (2, 3, 1, 0)[i]
        own = lambda d: u_ref.at[kof(d), half, r, :, ROWS[2], :]
        more = lambda d: d_ref.at[kof(d), r, :, ROWS[2], :]
        return ring8(own, adder(own, more), lambda j: rc1.at[j, r],
                     c1s, lambda j: c1r.at[j, r])

    def a2(i):
        ks = pl.ds(2 * i, 2)
        own = lambda r: u_ref.at[ks, half, 0, r, ROWS[0], :]
        return ring4(own, adder(own), lambda j: ra2.at[j, ks],
                     a2s, lambda j: a2r.at[j, i], qdev, direct=i in ())

    def b2(i):
        ks = pl.ds(2 * i, 2)
        own = lambda r: u_ref.at[ks, half, r, 0, ROWS[1], :]
        return ring4(own, adder(own), lambda j: rb2.at[j, ks],
                     b2s, lambda j: b2r.at[j, i], pdev, direct=i in ())

    def c2(i):
        ys = pl.ds(2 - 2 * i, 2)
        own = lambda r: u_ref.at[kme, half, r, ys, ROWS[2], :]
        return ring4(own, adder(own), lambda j: rc2.at[j, ys],
                     c2s, lambda j: c2r.at[j, i], pdev)

    def c3():
        own = lambda r: u_ref.at[kme, half, 0, r, ROWS[2], :]
        return ring4(own, adder(own), lambda j: rc3.at[j],
                     c3s, lambda j: c3r.at[j], qdev, direct=True)

    def a3():
        own = lambda d: u_ref.at[kof(d), half, 0, 0, ROWS[0], :]
        return ring8_short(own, adder(own), lambda j: ra3.at[j], a3s, lambda j: a3r.at[j])

    def b3():
        own = lambda d: u_ref.at[kof(d), half, 0, 0, ROWS[1], :]
        return ring8_short(own, adder(own), lambda j: rb3.at[j], b3s, lambda j: b3r.at[j])

    def spread(i):
        if i == 0:
            ccopy.wait()
        for j in range(3 * i, 3 * i + 3):
            v = 2.0 * c_v[:, j, :]
            v = pltpu.roll(jnp.concatenate([v, v, v, v], axis=1), 128 - 8 * quarter, 1)
            for s in range(8):
                r = (s * NH + j) * 24
                p_ref[0, r:r + NH, :] = jnp.broadcast_to(v[:, s:s + 1], (NH, 128))

    def bar():
        ocopy.wait()
        ccopy.start()
        for t in range(2, 4):
            wcopy(t).wait()
        pl.semaphore_wait(barrier, len(greet))

    def each(f, n):
        return [functools.partial(f, i) for i in range(n)]

    m0 = functools.partial(matmul, 0, 0, CHUNKS, True)
    m1 = [functools.partial(matmul, 1, 2 * i, 2 * i + 2, False) for i in range(4)]
    g0, g, cb = each(make_first, 2), each(make, 4), each(spread, 6)
    w0 = [[functools.partial(lambda h, c: dfirst(h, c).wait_recv(), h, c) for c in range(3)] for h in range(2)]
    wd = [[functools.partial(lambda k, c: dcopy(k, c).wait_recv(), k, c) for c in range(3)] for k in range(4)]
    ra, rb, rc = [a1(k) for k in range(8)], [b1(k) for k in range(8)], [c1(i) for i in range(4)]
    sa, sb, sc = [a2(i) for i in range(4)], [b2(i) for i in range(4)], [c2(i) for i in range(2)]
    ta, tb, tc = a3(), b3(), c3()
    for run in (
        m0, bar, g0[0], g0[1], g[1], w0[0][0], ra[0][1], ra[0][0], m1[0], w0[0][1], rb[0][0], rb[0][1], w0[0][2],
        rc[2][0], m1[1], rc[0][0], w0[1][0], ra[1][0], ra[1][1], m1[2], rc[1][0], w0[1][2], rc[3][0], wd[1][0],
        ra[2][0], ra[3][1], w0[1][1], rb[1][0], ra[3][0], m1[3], ra[0][2], g[2], wd[1][1], rb[2][0], wd[1][2],
        rb[2][1], rc[2][1], rc[0][2], rb[3][0], rc[1][1], rc[2][2], rb[1][1], wd[2][0], rc[0][1], ra[2][1], g[3],
        rb[3][1], ra[4][1], ra[4][0], wd[2][2], wd[2][1], rc[1][2], ra[5][1], rb[1][2], rb[3][2], rc[2][5], ra[2][2],
        ra[0][3], wd[3][0], ra[1][2], wd[3][2], rb[4][0], rb[5][0], rb[4][1], rb[2][2], wd[3][1], cb[0], rc[0][3],
        rc[3][2], ra[5][0], rb[0][2], rb[6][0], rb[7][0], cb[1], ra[3][2], ra[7][0], rc[2][3], rc[1][5], ra[2][3],
        rc[0][5], ra[1][3], rb[7][1], rb[4][2], ra[4][2], ra[5][2], ra[6][0], sa[0][0], rc[1][3], rc[3][1], rb[1][3],
        rc[1][6], rb[5][2], rb[0][3], ra[3][3], rb[3][3], rb[5][1], rb[6][2], rb[6][1], rc[0][4], cb[4], sb[0][0],
        rb[2][3], sa[1][0], rc[3][3], rb[7][2], sa[0][1], rb[4][3], sb[1][0], ra[7][2], sa[0][2], ra[4][3], ra[7][1],
        rc[0][6], ra[5][3], ra[6][1], rc[3][5], ra[6][2], rb[5][3], sb[2][0], sb[0][1], rc[1][4], rc[2][6], rc[2][4],
        sb[0][2], rc[3][4], sa[1][1], sa[1][2], sa[2][0], rb[7][3], rc[0][7], sc[1][0], cb[3], sb[1][2], cb[2],
        sb[1][1], rb[6][3], sc[0][0], sb[2][1], rc[3][6], sb[3][0], ra[7][3], ra[6][3], sa[3][0], sa[0][3], sb[2][2],
        sa[1][3], sa[2][2], ta[0], sa[2][1], cb[5], sb[0][3], tb[0], sb[3][1], rc[1][7], sa[3][1], sb[1][3], ta[1],
        tb[1], rc[2][7], sc[0][1], sc[1][2], sc[0][2], tb[2], sc[1][1], sb[3][2], ta[2], sa[3][2], sb[2][3], tb[3],
        rc[3][7], sa[2][3], ta[3], ta[4], sc[0][3], tc[0], tb[4], tc[1], sa[3][3], ta[5], sb[3][3], sc[1][3], tb[5],
        tb[6], tc[2], ta[6], tc[3], tb[7], ta[7],
    ):
        run()

    for s in range(8):
        acc = None
        for j in range(NH):
            r = s * NH + j
            term = p_ref[0, r * 24:r * 24 + NH, :] * u_ref[kme, half, 0, 0, r:r + 1, :]
            acc = term if acc is None else acc + term
        g_ref[s * NH:s * NH + NH, :] = acc
    for i in range(5):
        v = [g_ref[8 * t:8 * t + 8, :] for t in ((4 * i, 4 * i + 1, 4 * i + 2, 4 * i + 3) if i < 4 else (16, 17, 16, 17))]
        for d, u in enumerate(fold4(v)):
            pk[d, 8 * i:8 * i + 8, :] = u

    def kcopy(rel):
        dev = (partner, pairdev, diagdev)[rel]
        d = (par * 2 + 1 - core, (1 - par) * 2 + 1 - core, (1 - par) * 2 + core)[rel]
        return remote(pk.at[d], rk.at[rel], ks_s, ks_r.at[rel], dev)

    for rel in (2, 1, 0):
        kcopy(rel).start()

    def unpack(ref, q):
        for t in range(18):
            tile = ref[8 * (t // 4):8 * (t // 4) + 8, :]
            if t % 4:
                tile = pltpu.roll(tile, 128 - 32 * (t % 4), 1)
            t_ref[pl.ds(pl.multiple_of(q * 144 + t * 8, 8), 8), :] = tile

    unpack(pk.at[par * 2 + core], quarter)
    for rel, q in ((0, par * 2 + 1 - half), (1, (1 - par) * 2 + half), (2, 3 - quarter)):
        kcopy(rel).wait_recv()
        unpack(rk.at[rel], q)
    o_ref[...] = jnp.transpose(t_ref[...])[:32, :]
    for whole, sem in ((d_ref, ds_s), (ra1, a1s), (rb1, b1s), (rc1, c1s), (ra2, a2s), (rb2, b2s), (rc2, c2s),
                       (ra3, a3s), (rb3, b3s), (rc3, c3s), (rk, ks_s)):
        remote(whole, whole, sem, ks_r.at[0], partner).wait_send()


def shards(projectors, wavefunctions, coupling, atom_order):
    a = projectors.reshape(KLOC, NKB)
    w = wavefunctions.reshape(KLOC, BANDS)
    f32 = jnp.float32
    dma = pltpu.SemaphoreType.DMA
    any_spec = pl.BlockSpec(memory_space=pltpu.HBM)
    sems = []
    for shape in ((2, 8), (2, 8), (6, 4), (2, 4), (2, 4), (2, 2), (3,), (3,), (2,), (3,)):
        sems += [dma, dma(shape)]
    out = pl.pallas_call(
        kernel,
        out_shape=pltpu.VMEM((32, 576), f32),
        in_specs=[any_spec, any_spec, any_spec, any_spec],
        out_specs=pl.BlockSpec(memory_space=pltpu.VMEM),
        scratch_shapes=[
            pltpu.VMEM((2, NKB + 8, 128), f32),
            pltpu.VMEM((8, 2, 4, 4, 144, 128), f32),
            pltpu.VMEM((8, 4, 4, 144, 128), f32),
            pltpu.VMEM((KLOC, NKB), jnp.bfloat16),
            pltpu.VMEM((4, KLOC, 128), jnp.bfloat16),
            pltpu.VMEM((NH, NH, 32), f32),
            pltpu.VMEM((144, 128), f32),
            pltpu.VMEM((4, 40, 128), f32),
            pltpu.VMEM((3, 40, 128), f32),
            pltpu.VMEM((576, 128), f32),
            pltpu.VMEM((3, 8, 4, 48, 128), f32),
            pltpu.VMEM((3, 8, 4, 48, 128), f32),
            pltpu.VMEM((7, 4, 4, 48, 128), f32),
            pltpu.VMEM((3, 8, 48, 128), f32),
            pltpu.VMEM((3, 8, 48, 128), f32),
            pltpu.VMEM((3, 4, 48, 128), f32),
            pltpu.VMEM((7, 48, 128), f32),
            pltpu.VMEM((7, 48, 128), f32),
            pltpu.VMEM((3, 48, 128), f32),
            pltpu.SMEM((512,), jnp.int32),
            dma((5,)),
            dma((4,)),
            dma,
            dma,
            dma,
            dma((5, 3)),
        ] + sems,
        compiler_params=pltpu.CompilerParams(
            vmem_limit_bytes=62500000, collective_id=0, has_side_effects=True),
        cost_estimate=pl.CostEstimate(flops=2 * KLOC * NKB * BANDS, bytes_accessed=10 * 2**20, transcendentals=0),
    )(atom_order, a, w, coupling.transpose(1, 2, 0))
    return out.T


def solution(mesh):
    return jax.shard_map(
        shards,
        mesh=mesh,
        in_specs=(
            P(None, ("gr", "gc"), None),
            P(None, ("gr", "gc"), None),
            P("gc", None, None),
            P(),
        ),
        out_specs=P("gc", "gr"),
        check_vma=False,
    )
```

time: 67.2 us -> 63 us (0.938)
  Pallas kernels: 66.4 us -> 62.7 us
    pallas_call x1, Pallas kernels: 66.4 us -> 62.7 us  [shards(): pl.pallas_call(kernel, out_shape=pltpu.VMEM((32, 576), f32), in_specs=[an...]
where the time goes in v3:
time: 63 us; the launch traced here: 63.3 us
  Pallas kernels  62.7 us (100%)
  local copies, waits for them, and re-layouts  0.64 us (1%)
    pallas_call x1, Pallas kernels, shards(): pl.pallas_call(kernel, out_shape=pltpu.VMEM((32, 576), f32), in_specs=[an...  62.7 us

profile of v3, /device:TPU:1, one launch (start us, length us, event | category | flops | bytes accessed | tf_op | source)
XLA Modules:
  0.0 63.3 jit_solution(6542673707069197045)
XLA Ops:
  0.0 62.7 %shard_map.46 = f32[32,576]{1,0:T(8,128)S(1)} custom-call(s32[512]{0:T(512)} %order_hbm.1, bf16[512,9216]{1,0:T(8,128)(2,1)} %bitcast.5, bf16[512,512]{1,0:T(8,128)(2,1)} %bitcast.6, f32[18,18,32]{2,1,0:T(8,128)} %bitcast.7), custom_call_target="tpu_custom_call" | custom-call | flops 4831838208 | bytes 10485760 | tf_op jit(solution)/shard_map/pallas_call | solution.py:397
  62.7 0.6 %copy.6 = f32[576,32]{0,1:T(8,128)} copy(f32[576,32]{0,1:T(8,128)S(1)} %bitcast.4) | data formatting | bytes 147456

commit v4 on v3

--- a/solution.py
+++ b/solution.py
@@ -12,7 +12,7 @@
 BANDS = 512
 NKB = 9216
 KLOC = 512
-MC = 1152
+MC = 1536
 CHUNKS = NKB // MC
 ROWS = (slice(0, 48), slice(48, 96), slice(96, 144))
 
@@ -73,7 +73,7 @@
         odd = rel % 2
         up = rel // 2
         pos = odd * (1 + (par + up) % 2) + (1 - odd) * (3 - 3 * up)
-        return 2 * pos + (par + d + 8) % 2
+        return 2 * pos + (par + d + 8 + par * (1 - odd) * up) % 2
 
     kme = 6 + par
 
@@ -121,18 +121,21 @@
             p_ref[1, rows, :] = r[:, 128:]
 
     def gather(kk, zs):
-        @pl.loop(0, 16)
-        def _(g):
-            for zl in zs:
-                for h in range(2):
-                    way = 1 - 2 * h
-                    rx = (way * (g // 4 - x) + 4) % 4
-                    ry = (way * (g % 4 - y) + 4) % 4
-                    p, q = (rx, ry) if h == 0 else (ry, rx)
-                    for s in range(8):
-                        start = order[g * 32 + (2 * zl + h) * 8 + s] * NH
-                        n = 24 if s < 7 else 18
-                        u_ref[2 * kk + zl, h, p, q, s * 18:s * 18 + n, :] = p_ref[kk % 2, pl.ds(start, n), :]
+        step = 1
+
+        @pl.loop(0, 16 // step)
+        def _(i):
+            for g in [i * step + j for j in range(step)]:
+                for k, zl in zs:
+                    for h in range(2):
+                        way = 1 - 2 * h
+                        rx = (way * (g // 4 - x) + 4) % 4
+                        ry = (way * (g % 4 - y) + 4) % 4
+                        p, q = (rx, ry) if h == 0 else (ry, rx)
+                        for s in range(8):
+                            start = order[g * 32 + (2 * zl + h) * 8 + s] * NH
+                            n = 24 if s < 7 else 18
+                            u_ref[2 * kk + k, h, p, q, s * 18:s * 18 + n, :] = p_ref[kk % 2, pl.ds(start, n), :]
 
     def remote(src, dst, ssem, rsem, dev):
         return pltpu.make_async_remote_copy(src_ref=src, dst_ref=dst, send_sem=ssem, recv_sem=rsem,
@@ -144,18 +147,19 @@
                       ds_s, ds_r.at[kk, c], partner)
 
     def dfirst(h, c):
-        k = (par + h) % 2
-        return remote(u_ref.at[k, 1 - half, :, :, ROWS[c], :], d_ref.at[k, :, :, ROWS[c], :],
+        return remote(u_ref.at[h, 1 - half, :, :, ROWS[c], :], d_ref.at[h, :, :, ROWS[c], :],
                       ds_s, ds_r.at[4 * h, c], partner)
 
     def make(kk):
-        gather(kk, (0, 1))
-        for c in (0, 2, 1):
+        gather(kk, ((0, 0), (1, 1)))
+        if kk == 3:
+            ccopy.wait()
+        for c in (0, 1, 2):
             dcopy(kk, c).start()
 
     def make_first(h):
-        gather(0, ((par + h) % 2,))
-        for c in (0, 2, 1):
+        gather(0, ((h, (par + h) % 2),))
+        for c in (0, 1, 2):
             dfirst(h, c).start()
 
     def ring4(own, add, slot, ssem, rsem, dev, direct=False):
@@ -248,16 +252,14 @@
         return add
 
     def a1(k):
-        at = (par + k) % 2 if k < 2 else k
-        own = lambda r: u_ref.at[at, half, r, :, ROWS[0], :]
-        more = lambda r: d_ref.at[at, r, :, ROWS[0], :]
+        own = lambda r: u_ref.at[k, half, r, :, ROWS[0], :]
+        more = lambda r: d_ref.at[k, r, :, ROWS[0], :]
         return ring4(own, adder(own, more), lambda j: ra1.at[j, k],
                      a1s, lambda j: a1r.at[j, k], pdev)
 
     def b1(k):
-        at = (par + k) % 2 if k < 2 else k
-        own = lambda r: u_ref.at[at, half, :, r, ROWS[1], :]
-        more = lambda r: d_ref.at[at, :, r, ROWS[1], :]
+        own = lambda r: u_ref.at[k, half, :, r, ROWS[1], :]
+        more = lambda r: d_ref.at[k, :, r, ROWS[1], :]
         return ring4(own, adder(own, more), lambda j: rb1.at[j, k],
                      b1s, lambda j: b1r.at[j, k], qdev)
 
@@ -272,13 +274,13 @@
         ks = pl.ds(2 * i, 2)
         own = lambda r: u_ref.at[ks, half, 0, r, ROWS[0], :]
         return ring4(own, adder(own), lambda j: ra2.at[j, ks],
-                     a2s, lambda j: a2r.at[j, i], qdev, direct=i in ())
+                     a2s, lambda j: a2r.at[j, i], qdev, direct=i in (3,))
 
     def b2(i):
         ks = pl.ds(2 * i, 2)
         own = lambda r: u_ref.at[ks, half, r, 0, ROWS[1], :]
         return ring4(own, adder(own), lambda j: rb2.at[j, ks],
-                     b2s, lambda j: b2r.at[j, i], pdev, direct=i in ())
+                     b2s, lambda j: b2r.at[j, i], pdev, direct=i in (3,))
 
     def c2(i):
         ys = pl.ds(2 - 2 * i, 2)
@@ -300,8 +302,6 @@
         return ring8_short(own, adder(own), lambda j: rb3.at[j], b3s, lambda j: b3r.at[j])
 
     def spread(i):
-        if i == 0:
-            ccopy.wait()
         for j in range(3 * i, 3 * i + 3):
             v = 2.0 * c_v[:, j, :]
             v = pltpu.roll(jnp.concatenate([v, v, v, v], axis=1), 128 - 8 * quarter, 1)
@@ -320,7 +320,7 @@
         return [functools.partial(f, i) for i in range(n)]
 
     m0 = functools.partial(matmul, 0, 0, CHUNKS, True)
-    m1 = [functools.partial(matmul, 1, 2 * i, 2 * i + 2, False) for i in range(4)]
+    m1 = [functools.partial(matmul, 1, 2 * i, 2 * i + 2, False) for i in range(3)]
     g0, g, cb = each(make_first, 2), each(make, 4), each(spread, 6)
     w0 = [[functools.partial(lambda h, c: dfirst(h, c).wait_recv(), h, c) for c in range(3)] for h in range(2)]
     wd = [[functools.partial(lambda k, c: dcopy(k, c).wait_recv(), k, c) for c in range(3)] for k in range(4)]
@@ -328,23 +328,23 @@
     sa, sb, sc = [a2(i) for i in range(4)], [b2(i) for i in range(4)], [c2(i) for i in range(2)]
     ta, tb, tc = a3(), b3(), c3()
     for run in (
-        m0, bar, g0[0], g0[1], g[1], w0[0][0], ra[0][1], ra[0][0], m1[0], w0[0][1], rb[0][0], rb[0][1], w0[0][2],
-        rc[2][0], m1[1], rc[0][0], w0[1][0], ra[1][0], ra[1][1], m1[2], rc[1][0], w0[1][2], rc[3][0], wd[1][0],
-        ra[2][0], ra[3][1], w0[1][1], rb[1][0], ra[3][0], m1[3], ra[0][2], g[2], wd[1][1], rb[2][0], wd[1][2],
-        rb[2][1], rc[2][1], rc[0][2], rb[3][0], rc[1][1], rc[2][2], rb[1][1], wd[2][0], rc[0][1], ra[2][1], g[3],
-        rb[3][1], ra[4][1], ra[4][0], wd[2][2], wd[2][1], rc[1][2], ra[5][1], rb[1][2], rb[3][2], rc[2][5], ra[2][2],
-        ra[0][3], wd[3][0], ra[1][2], wd[3][2], rb[4][0], rb[5][0], rb[4][1], rb[2][2], wd[3][1], cb[0], rc[0][3],
-        rc[3][2], ra[5][0], rb[0][2], rb[6][0], rb[7][0], cb[1], ra[3][2], ra[7][0], rc[2][3], rc[1][5], ra[2][3],
-        rc[0][5], ra[1][3], rb[7][1], rb[4][2], ra[4][2], ra[5][2], ra[6][0], sa[0][0], rc[1][3], rc[3][1], rb[1][3],
-        rc[1][6], rb[5][2], rb[0][3], ra[3][3], rb[3][3], rb[5][1], rb[6][2], rb[6][1], rc[0][4], cb[4], sb[0][0],
-        rb[2][3], sa[1][0], rc[3][3], rb[7][2], sa[0][1], rb[4][3], sb[1][0], ra[7][2], sa[0][2], ra[4][3], ra[7][1],
-        rc[0][6], ra[5][3], ra[6][1], rc[3][5], ra[6][2], rb[5][3], sb[2][0], sb[0][1], rc[1][4], rc[2][6], rc[2][4],
-        sb[0][2], rc[3][4], sa[1][1], sa[1][2], sa[2][0], rb[7][3], rc[0][7], sc[1][0], cb[3], sb[1][2], cb[2],
-        sb[1][1], rb[6][3], sc[0][0], sb[2][1], rc[3][6], sb[3][0], ra[7][3], ra[6][3], sa[3][0], sa[0][3], sb[2][2],
-        sa[1][3], sa[2][2], ta[0], sa[2][1], cb[5], sb[0][3], tb[0], sb[3][1], rc[1][7], sa[3][1], sb[1][3], ta[1],
-        tb[1], rc[2][7], sc[0][1], sc[1][2], sc[0][2], tb[2], sc[1][1], sb[3][2], ta[2], sa[3][2], sb[2][3], tb[3],
-        rc[3][7], sa[2][3], ta[3], ta[4], sc[0][3], tc[0], tb[4], tc[1], sa[3][3], ta[5], sb[3][3], sc[1][3], tb[5],
-        tb[6], tc[2], ta[6], tc[3], tb[7], ta[7],
+        m0, bar, g0[0], g0[1], w0[0][0], ra[0][0], ra[0][1], g[1], w0[0][2], w0[0][1], rc[0][0], rb[0][1], rc[3][0],
+        rb[0][0], rc[2][0], w0[1][0], ra[1][0], ra[1][1], m1[0], w0[1][1], rb[1][0], rb[1][1], m1[1], ra[0][2],
+        wd[1][0], ra[3][1], w0[1][2], rc[1][0], ra[3][0], ra[2][1], m1[2], wd[1][1], rb[2][0], rb[3][0], ra[2][0],
+        wd[1][2], rc[0][2], g[2], rc[0][1], rb[0][2], ra[1][2], rb[2][1], rb[1][2], rc[3][1], rb[3][1], rc[1][2],
+        g[3], rc[2][1], rc[1][1], wd[2][0], cb[4], cb[2], ra[5][1], wd[2][1], rb[4][0], ra[4][0], ra[2][2], ra[0][3],
+        wd[2][2], rb[5][0], rb[3][2], rc[3][2], cb[1], ra[5][0], ra[1][3], rc[0][5], wd[3][0], rb[0][3], wd[3][1],
+        ra[3][2], rc[2][2], rc[0][3], rb[7][0], rb[1][3], sb[0][0], cb[0], wd[3][2], rc[1][3], ra[7][0], rb[5][1],
+        rb[4][1], rb[4][2], rc[1][5], rb[2][2], rb[5][2], ra[5][2], ra[3][3], rc[2][3], rc[2][5], ra[4][1], rc[3][3],
+        ra[4][2], sa[0][0], ra[7][1], ra[2][3], ra[6][0], rc[1][6], rc[0][4], rb[3][3], sb[0][2], rb[2][3], sa[1][0],
+        sa[0][1], ra[7][2], sb[0][1], sb[1][0], ra[6][1], rc[0][6], rb[6][0], ra[5][3], ra[4][3], sa[1][1], rb[6][1],
+        rb[5][3], rb[4][3], cb[5], sb[2][0], sa[2][0], rb[7][1], sa[0][2], rc[1][4], rb[7][2], sa[1][2], rc[3][5],
+        ra[6][2], rc[2][6], rb[6][2], rc[2][4], sa[2][2], rc[0][7], rc[3][4], sc[0][0], sb[1][2], sb[1][1], ra[7][3],
+        sb[2][1], sb[2][2], sc[1][0], sa[0][3], sb[0][3], ta[0], tb[0], rc[1][7], sa[2][1], sa[1][3], cb[3], sc[0][1],
+        ta[1], rc[3][6], ra[6][3], sa[3][0], sa[3][1], sa[3][2], rb[7][3], rb[6][3], sb[3][0], ta[2], sb[1][3],
+        sc[1][1], sb[3][1], rc[2][7], tb[2], sc[0][2], tb[1], sb[3][2], sa[2][3], ta[3], sb[2][3], tb[3], sc[1][2],
+        ta[4], rc[3][7], tb[4], sc[0][3], tc[1], tc[0], sa[3][3], ta[5], sb[3][3], tb[5], ta[6], sc[1][3], tc[2],
+        tb[6], ta[7], tc[3], tb[7],
     ):
         run()
 

time: 63 us -> 60 us (0.952)
  Pallas kernels: 62.7 us -> 59.3 us
    pallas_call x1, Pallas kernels: 62.7 us -> 59.3 us  [shards(): pl.pallas_call(kernel, out_shape=pltpu.VMEM((32, 576), f32), in_specs=[an...]
where the time goes in v4:
time: 60 us; the launch traced here: 59.9 us
  Pallas kernels  59.3 us (99%)
  local copies, waits for them, and re-layouts  0.64 us (1%)
    pallas_call x1, Pallas kernels, shards(): pl.pallas_call(kernel, out_shape=pltpu.VMEM((32, 576), f32), in_specs=[an...  59.3 us

profile of v4, /device:TPU:1, one launch (start us, length us, event | category | flops | bytes accessed | tf_op | source)
XLA Modules:
  0.0 59.9 jit_solution(16862486545748842995)
XLA Ops:
  0.0 59.3 %shard_map.46 = f32[32,576]{1,0:T(8,128)S(1)} custom-call(s32[512]{0:T(512)} %order_hbm.1, bf16[512,9216]{1,0:T(8,128)(2,1)} %bitcast.5, bf16[512,512]{1,0:T(8,128)(2,1)} %bitcast.6, f32[18,18,32]{2,1,0:T(8,128)} %bitcast.7), custom_call_target="tpu_custom_call" | custom-call | flops 4831838208 | bytes 10485760 | tf_op jit(solution)/shard_map/pallas_call | solution.py:397
  59.3 0.6 %copy.6 = f32[576,32]{0,1:T(8,128)} copy(f32[576,32]{0,1:T(8,128)S(1)} %bitcast.4) | data formatting | bytes 147456

commit v5 on v4

--- a/solution.py
+++ b/solution.py
@@ -344,21 +344,26 @@
         ta[1], rc[3][6], ra[6][3], sa[3][0], sa[3][1], sa[3][2], rb[7][3], rb[6][3], sb[3][0], ta[2], sb[1][3],
         sc[1][1], sb[3][1], rc[2][7], tb[2], sc[0][2], tb[1], sb[3][2], sa[2][3], ta[3], sb[2][3], tb[3], sc[1][2],
         ta[4], rc[3][7], tb[4], sc[0][3], tc[1], tc[0], sa[3][3], ta[5], sb[3][3], tb[5], ta[6], sc[1][3], tc[2],
-        tb[6], ta[7], tc[3], tb[7],
+        tb[6], ta[7], tc[3],
     ):
         run()
 
-    for s in range(8):
-        acc = None
-        for j in range(NH):
-            r = s * NH + j
-            term = p_ref[0, r * 24:r * 24 + NH, :] * u_ref[kme, half, 0, 0, r:r + 1, :]
-            acc = term if acc is None else acc + term
-        g_ref[s * NH:s * NH + NH, :] = acc
-    for i in range(5):
-        v = [g_ref[8 * t:8 * t + 8, :] for t in ((4 * i, 4 * i + 1, 4 * i + 2, 4 * i + 3) if i < 4 else (16, 17, 16, 17))]
-        for d, u in enumerate(fold4(v)):
-            pk[d, 8 * i:8 * i + 8, :] = u
+    def couple(slots, groups):
+        for s in slots:
+            acc = None
+            for j in range(NH):
+                r = s * NH + j
+                term = p_ref[0, r * 24:r * 24 + NH, :] * u_ref[kme, half, 0, 0, r:r + 1, :]
+                acc = term if acc is None else acc + term
+            g_ref[s * NH:s * NH + NH, :] = acc
+        for i in groups:
+            v = [g_ref[8 * t:8 * t + 8, :] for t in ((4 * i, 4 * i + 1, 4 * i + 2, 4 * i + 3) if i < 4 else (16, 17, 16, 17))]
+            for d, u in enumerate(fold4(v)):
+                pk[d, 8 * i:8 * i + 8, :] = u
+
+    couple((0, 1, 6, 7), (0, 4))
+    tb[7]()
+    couple((2, 3, 4, 5), (1, 2, 3))
 
     def kcopy(rel):
         dev = (partner, pairdev, diagdev)[rel]

time: 60 us -> 59.9 us (level)
  no operation moved by 1% of the time
where the time goes in v5:
time: 59.9 us; the launch traced here: 59.8 us
  Pallas kernels  59.2 us (99%)
  local copies, waits for them, and re-layouts  0.64 us (1%)
    pallas_call x1, Pallas kernels, shards(): pl.pallas_call(kernel, out_shape=pltpu.VMEM((32, 576), f32), in_specs=[an...  59.2 us

profile of v5, /device:TPU:1, one launch (start us, length us, event | category | flops | bytes accessed | tf_op | source)
XLA Modules:
  0.0 59.8 jit_solution(3823434537237234198)
XLA Ops:
  0.0 59.2 %shard_map.46 = f32[32,576]{1,0:T(8,128)S(1)} custom-call(s32[512]{0:T(512)} %order_hbm.1, bf16[512,9216]{1,0:T(8,128)(2,1)} %bitcast.5, bf16[512,512]{1,0:T(8,128)(2,1)} %bitcast.6, f32[18,18,32]{2,1,0:T(8,128)} %bitcast.7), custom_call_target="tpu_custom_call" | custom-call | flops 4831838208 | bytes 10485760 | tf_op jit(solution)/shard_map/pallas_call | solution.py:402
  59.2 0.6 %copy.6 = f32[576,32]{0,1:T(8,128)} copy(f32[576,32]{0,1:T(8,128)S(1)} %bitcast.4) | data formatting | bytes 147456
